TPU v7x, 8 devices: a whole 2x2x1 slice. The times are simulated.
8 devices in a mesh: data: 8 (over z, y, x, core).
Axes of the slice: x: 2, y: 2, z: 1, core: 2. Of those that a mesh axis runs over, the one named last changes fastest.
Arguments:
- tokens: bfloat16 [65536, 256], P('data')
- out_grad: bfloat16 [65536, 256], P('data')
- w_up: bfloat16 [2, 256, 1024], replicated
- w_down: bfloat16 [2, 1024, 256], replicated
- a_up_old: float32 [2, 256, 256], replicated
- s_up_old: float32 [2, 1024, 1024], replicated
- a_down_old: float32 [2, 1024, 1024], replicated
- s_down_old: float32 [2, 256, 256], replicated
- a_up_inv: float32 [2, 256, 256], replicated
- s_up_inv: float32 [2, 1024, 1024], replicated
- a_down_inv: float32 [2, 1024, 1024], replicated
- s_down_inv: float32 [2, 256, 256], replicated
- factor_decay: float32 [], replicated
Outputs:
- output 1: float32 [2, 256, 1024], replicated
- output 2: float32 [2, 1024, 256], replicated
- output 3: float32 [2, 256, 256], replicated
- output 4: float32 [2, 1024, 1024], replicated
- output 5: float32 [2, 1024, 1024], replicated
- output 6: float32 [2, 256, 256], replicated
All inputs are finite; a program needn't handle non-finite values.
Results may differ from a plain program's by a relative error of at most 0.00171.
Values are sent between devices in bfloat16 or wider.
A program may use at most 1 GiB of HBM per device.

v0:
```python
import functools

import jax
import jax.numpy as jnp
from jax import lax
from jax.experimental import pallas as pl
from jax.experimental.pallas import tpu as pltpu
from jax.sharding import PartitionSpec as P

F32 = jnp.float32
BF16 = jnp.bfloat16
MESH = pl.DeviceIdType.MESH
HIGHEST = lax.Precision.HIGHEST
PIECE = 32

D = 256
FF = 1024
TILE = 512
C0 = 0.7978845608028654
C1 = C0 * 0.044715

AU0, SD1, AD0, AU1, AD1, DD1, DU1, SU1, SD0, DU0, DD0, SU0 = 0, 1, 2, 11, 12, 21, 25, 29, 38, 39, 43, 47
BLOCKS = 56
AU = (AU0, AU1)
SD = (SD0, SD1)
AD = (AD0, AD1)
SU = (SU0, SU1)
DU = (DU0, DU1)
DD = (DD0, DD1)
ABOVE = ((0, 1), (0, 2), (1, 2), (0, 3), (1, 3), (2, 3))
LAST = ((0, 0), (0, 1), (1, 1))
COLUMNS = ((0, 1), (2,), (3,), ())

UNITS = ((0, 11, 0), (11, 10, 11), (21, 4, 21), (25, 4, 25), (29, 9, 0), (38, 5, 11), (43, 4, 16), (47, 3, 21), (50, 3, 24), (53, 3, 27))
POOL = 30

AFTER_1 = ((0, 0),)
PLAN_2A = ((1, 0, 1), (5, 0, 2), (8, 0, 3), (11, 0, 4))
AFTER_2A = ((1, 0), (3, 0), (2, 0))
PLAN_2B = ((0, 0, 5), (2, 1, 1), (3, 3, 1), (3, 2, 1), (5, 0, 6))
AFTER_2B = ((4, 0),)
PLAN_3A = ((0, 1, 2), (2, 4, 1), (3, 3, 2), (4, 1, 3), (5, 2, 2), (6, 4, 2), (7, 3, 3), (8, 1, 4), (8, 2, 3), (9, 4, 3), (10, 3, 4), (11, 1, 5), (13, 2, 4), (14, 1, 6), (14, 4, 4))
AFTER_3A = ((5, 0), (6, 0))
PLAN_3B = ((1, 3, 5), (2, 6, 1), (3, 5, 1), (3, 3, 6), (3, 2, 5), (6, 6, 2), (6, 2, 6))
AFTER_3B = ((8, 0), (9, 0), (7, 0))
TAIL = ((5, 2), (8, 1), (7, 1), (6, 3), (8, 2), (9, 1), (5, 3), (8, 3), (7, 2), (9, 2), (6, 4), (5, 4), (7, 3), (9, 3), (8, 4), (6, 5), (6, 6), (5, 5), (9, 4), (5, 6), (4, 5), (7, 4), (4, 6), (8, 5), (9, 5), (8, 6), (9, 6), (7, 5), (7, 6))


def block_kinds():
    kinds = {}
    for b in range(2):
        for m, base in enumerate((AD[b], SU[b])):
            for k, (i, j) in enumerate(ABOVE):
                kinds[base + k] = ("above", m, b, i, j)
            for k in range(3):
                kinds[base + 6 + k] = ("diagonal", m, b, k, k)
        kinds[AU[b]] = ("small", 0, b, 0, 0)
        kinds[SD[b]] = ("small", 1, b, 0, 0)
    return kinds


KINDS = block_kinds()


def nn(a, b, precision=None):
    return lax.dot_general(a, b, (((1,), (0,)), ((), ())), preferred_element_type=F32, precision=precision)


def nt(a, b):
    return lax.dot_general(a, b, (((1,), (1,)), ((), ())), preferred_element_type=F32)


def half_gelu(z):
    sq = z * z
    return sq, jnp.tanh(z * (C1 * sq + C0)) * 0.5 + 0.5


def main_kernel(rows, batch_total,
                tok_hbm, grad_hbm, wup, wdn, rho_ref, a_up_old, s_up_old, a_down_old, s_down_old, s_up_inv, a_down_inv,
                acc, g_hbm, tok, grad, wup_t, wdn_t, u1_t, e1_t, hg, z_part, dh_part, left, big_old, corner_old, small_old, inv,
                r0, r1, r2, tok_sem, grad_sem, old_sem, inv_sem, g_sem, send_sem, recv_sem, sent_sem):
    tiles = rows // TILE
    me = lax.axis_index("data")
    core = lax.rem(me, 2)
    xpos = lax.rem(me // 2, 2)
    ypos = me // 4
    core_peer = me + 1 - 2 * core
    x_peer = me + 2 - 4 * xpos
    y_peer = me + 4 - 8 * ypos

    barrier = pltpu.get_barrier_semaphore()
    for peer in (core_peer, x_peer, y_peer):
        pl.semaphore_signal(barrier, inc=1, device_id=(peer,), device_id_type=MESH)

    def tok_copy(i):
        ds = pl.ds(i * TILE, TILE)
        return pltpu.make_async_copy(tok_hbm.at[ds, :], tok.at[ds, :], tok_sem.at[i])

    def grad_copy(i):
        ds = pl.ds(i * TILE, TILE)
        return pltpu.make_async_copy(grad_hbm.at[ds, :], grad.at[ds, :], grad_sem.at[i])

    for i in range(tiles):
        tok_copy(i).start()
        grad_copy(i).start()

    half = core * 128
    a_half = half + xpos * 32
    b_half = half + 64 + ypos * 32
    own_a = a_half + ypos * 16
    own_b = b_half + xpos * 16
    own = (own_a, own_b)

    for m, old in enumerate((a_down_old, s_up_old)):
        for b in range(2):
            for i in range(3):
                for p in range(2):
                    dst = pl.ds(p * 16, 16)
                    pltpu.make_async_copy(old.at[b, pl.ds(i * 256 + own[p], 16), :],
                                          big_old.at[m, b, i, dst, :], old_sem.at[0]).start()
                    row = i * 256 + own[p] + core * (768 + 128 * LAST[i][0] - 128 - i * 256)
                    col = i * 256 + core * (768 + 128 * LAST[i][1] - i * 256)
                    pltpu.make_async_copy(old.at[b, pl.ds(pl.multiple_of(row, 16), 16), pl.ds(pl.multiple_of(col, 128), 128)],
                                          corner_old.at[m, b, i, dst, :], old_sem.at[2]).start()
    for m, old in enumerate((a_up_old, s_down_old)):
        for b in range(2):
            for p in range(2):
                pltpu.make_async_copy(old.at[b, pl.ds(own[p], 16), :],
                                      small_old.at[m, b, pl.ds(p * 16, 16), :], old_sem.at[1]).start()

    def inv_copy(slot, b):
        return pltpu.make_async_copy((s_up_inv, a_down_inv)[slot].at[b], inv.at[slot], inv_sem.at[slot])

    for slot in range(2):
        inv_copy(slot, 1).start()

    acc[...] = jnp.zeros_like(acc)
    for b in range(2):
        wup_t[b] = wup[b].T
    wdn_t[...] = wdn[0].T

    def remote(u, slot, src, dst, peer):
        return pltpu.make_async_remote_copy(src_ref=src, dst_ref=dst, send_sem=send_sem.at[u, slot],
                                            recv_sem=recv_sem.at[u, slot], device_id=(peer,), device_id_type=MESH)

    def exchange(u, stage):
        b0, n, p0 = UNITS[u]
        blk = pl.ds(b0, n)
        pool = pl.ds(p0, n)

        def at(row, count):
            return acc.at[blk, pl.ds(pl.multiple_of(row, 16), count), :]

        if stage == 0:
            return [remote(u, 0, at((1 - core) * 128, 128), r0.at[pool], core_peer)]
        if stage == 1:
            return [remote(u, 1, at(half + (1 - xpos) * 32, 32), r1.at[0, pool], x_peer),
                    remote(u, 2, at(half + 64 + (1 - ypos) * 32, 32), r1.at[1, pool], y_peer)]
        if stage == 2:
            return [remote(u, 3, at(a_half + (1 - ypos) * 16, 16), r2.at[0, pool], y_peer),
                    remote(u, 4, at(b_half + (1 - xpos) * 16, 16), r2.at[1, pool], x_peer)]
        if stage == 3:
            return [remote(u, 5, at(own_a, 16), at(own_a, 16), y_peer),
                    remote(u, 6, at(own_b, 16), at(own_b, 16), x_peer)]
        if stage == 4:
            return [remote(u, 7, at(a_half, 32), at(a_half, 32), x_peer),
                    remote(u, 8, at(b_half, 32), at(b_half, 32), y_peer)]
        return [remote(u, 9, at(half, 128), at(half, 128), core_peer)]

    slots = {0: [(0, core_peer)], 1: [(1, x_peer), (2, y_peer)], 2: [(3, y_peer), (4, x_peer)]}

    def start(u, stage):
        if stage >= 3:
            for slot, _ in slots[5 - stage]:
                pl.semaphore_wait(sent_sem.at[u, slot], 1)
        for copy in exchange(u, stage):
            copy.start()

    def finish(u, stage):
        for copy in exchange(u, stage):
            copy.wait()
        if stage < 3:
            for slot, peer in slots[stage]:
                pl.semaphore_signal(sent_sem.at[u, slot], inc=1, device_id=(peer,), device_id_type=MESH)

    def add_rows(u, row, count, buf, lead):
        b0, n, p0 = UNITS[u]
        ds = pl.ds(pl.multiple_of(row, 16), count)

        def body(k, carry):
            acc[b0 + k, ds, :] += buf[lead + (p0 + k,)]
            return carry

        lax.fori_loop(0, n, body, 0)

    def factor_update(u):
        b0, n, _ = UNITS[u]
        rho = rho_ref[0, 0]
        fresh = (1.0 - rho) * (1.0 / batch_total)
        for k in range(b0, b0 + n):
            if k not in KINDS:
                continue
            kind, m, b, i, j = KINDS[k]
            for p in range(2):
                ds = pl.ds(pl.multiple_of(own[p], 16), 16)
                if kind == "small":
                    parts = [(slice(0, 256), small_old[m, b, p * 16:p * 16 + 16, :])]
                elif kind == "above":
                    parts = [(slice(0, 256), big_old[m, b, i, p * 16:p * 16 + 16, j * 256:j * 256 + 256])]
                else:
                    parts = [(slice(0, 128), corner_old[m, b, i, p * 16:p * 16 + 16, :]),
                             (slice(128, 256), big_old[m, b, i, p * 16:p * 16 + 16, i * 256 + 128:i * 256 + 256])]
                for cols, old in parts:
                    acc[k, ds, cols] = rho * old + fresh * acc[k, ds, cols]

    def wide_product(first, slot):
        ds = [pl.ds(pl.multiple_of(own[p], 16), 16) for p in range(2)]
        for j in range(4):
            for p in range(2):
                left[p * 16:p * 16 + 16, j * 256:j * 256 + 256] = acc[first + j, ds[p], :] * (1.0 / batch_total)

        def body(j, carry):
            prod = nn(left[...], inv[slot, :, pl.ds(pl.multiple_of(j * 256, 256), 256)], HIGHEST)
            for p in range(2):
                acc[first + j, ds[p], :] = prod[p * 16:p * 16 + 16, :]
            return carry

        lax.fori_loop(0, 4, body, 0)

    def post(u):
        b0, n, _ = UNITS[u]
        factor_update(u)
        for b in (1, 0):
            for slot, first in enumerate((DU[b], DD[b])):
                if b0 <= first < b0 + n:
                    inv_copy(slot, b).wait()
                    wide_product(first, slot)
                    if b == 1:
                        inv_copy(slot, 0).start()

    def advance(u, step):
        if step == 0:
            start(u, 0)
            return
        finish(u, step - 1)
        if step == 1:
            add_rows(u, half, 128, r0, ())
        elif step == 2:
            add_rows(u, a_half, 32, r1, (0,))
            add_rows(u, b_half, 32, r1, (1,))
        elif step == 3:
            add_rows(u, own_a, 16, r2, (0,))
            add_rows(u, own_b, 16, r2, (1,))
            post(u)
        if step < 6:
            start(u, step)

    def ticks(m, plan, per_step=1, k=0):
        for t in sorted(set(t for t, _, _ in plan)):
            if t % per_step != k:
                continue

            @pl.when(m == t // per_step)
            def _():
                for when, u, step in plan:
                    if when == t:
                        advance(u, step)

    def add_column(base, refs, j, lo=0):
        prod = sum(nt(ref[lo * 256:j * 256 + 256, :], ref[j * 256:j * 256 + 256, :]) for ref in refs)
        for i in range(lo, j):
            acc[base + ABOVE.index((i, j))] += prod[(i - lo) * 256:(i - lo) * 256 + 256, :]
        prod = prod[(j - lo) * 256:(j - lo) * 256 + 256, :]
        if j < 3:
            acc[base + 6 + j, 0:128, :] += prod[0:128, :]
            acc[base + 6 + j, 128:256, 128:256] += prod[128:256, 128:256]
        else:
            for k, (m, n) in enumerate(LAST):
                acc[base + 6 + k, 128:256, 0:128] += prod[m * 128:m * 128 + 128, n * 128:n * 128 + 128]

    def symmetric_part(base, ref, r):
        return [functools.partial(add_column, base, [ref], j) for j in COLUMNS[r]]

    def rectangle_part(base, left, ref, r):
        def add():
            acc[base + r] += nt(left(), ref[r * 256:r * 256 + 256, :])

        return [add]

    def square_part(base, x):
        def add():
            acc[base] += nt(x(), x())

        return [add]

    def activation_part(b, r, u_t, q_t, h, g):
        z_ref, dh_ref = z_part.at[r % 2], dh_part.at[r % 2]

        def products():
            z_ref[...] = nn(wup_t[b, r * 256:r * 256 + 256, :], u_t()).astype(BF16)
            if g is not None:
                dh_ref[...] = nn(wdn[b, r * 256:r * 256 + 256, :], q_t()).astype(BF16)

        def piece(k):
            rows_in = slice(k * PIECE, k * PIECE + PIECE)
            rows_out = slice(r * 256 + k * PIECE, r * 256 + k * PIECE + PIECE)
            z = z_ref[rows_in, :].astype(F32)
            sq, s = half_gelu(z)
            if h is not None:
                h[rows_out, :] = (z * s).astype(BF16)
            if g is not None:
                slope = s + (z * (s - s * s)) * (6 * C1 * sq + 2 * C0)
                g[rows_out, :] = (dh_ref[rows_in, :].astype(F32) * slope).astype(BF16)

        return [products] + [functools.partial(piece, k) for k in range(256 // PIECE)]

    def ahead(quarters):
        order = [quarters[0][0]]
        for r in range(4):
            if r < 3:
                order.append(quarters[r + 1][0])
            order += quarters[r][1:]
        return order

    def interleave(one, two):
        order = sorted([((k + 0.5) / len(one), 0, k) for k in range(len(one))]
                       + [((k + 0.5) / len(two), 1, k) for k in range(len(two))])
        for _, which, k in order:
            (one, two)[which][k]()

    def tile_slice(i):
        return pl.ds(pl.multiple_of(i * TILE, TILE), TILE)

    def row_pass(first, second, plan, begin=None, store=False):
        pairs = ((hg.at[0], hg.at[2]), (hg.at[1], hg.at[3]))

        def out(i, k):
            return pltpu.make_async_copy(pairs[k][1], g_hbm.at[i], g_sem.at[k])

        if begin is not None:
            begin(0)
        for r in range(4):
            for part in first(0, r, *pairs[0]):
                part()

        def body(m, carry):
            for k in range(2):
                i = 2 * m + k
                nxt = i + 1 if k == 0 else jnp.minimum(i + 1, tiles - 2)
                if store:
                    out(i, k).start()
                if begin is not None:
                    begin(i + 1)
                one = [first(nxt, r, *pairs[1 - k]) for r in range(4)]
                one = ahead(one)
                two = [part for r in range(4) for part in second(i, r, *pairs[k])]
                interleave(one, two)
                if store:
                    out(i, k).wait()
                ticks(m, plan, 2, k)
            return carry

        lax.fori_loop(0, tiles // 2, body, 0)

    def column(ref, i):
        return lambda: ref[:, tile_slice(i)]

    def turned(ref, i):
        return lambda: ref[tile_slice(i), :].T

    def pass_1():
        def begin(i):
            @pl.when(i < tiles)
            def _():
                tok_copy(i).wait()
                grad_copy(i).wait()

        def first(i, r, h, g):
            return activation_part(0, r, turned(tok, i), None, h, None)

        def second(i, r, h, g):
            def down():
                u1_t[:, tile_slice(i)] = nn(wdn_t[...], h[...]).astype(BF16)

            extra = ([down], square_part(AU0, turned(tok, i)), square_part(SD1, turned(grad, i)), [])[r]
            return extra + symmetric_part(AD0, h, r)

        row_pass(first, second, (), begin)

    def pass_2a():
        def first(i, r, h, g):
            return activation_part(1, r, column(u1_t, i), turned(grad, i), h, g)

        def second(i, r, h, g):
            def up():
                e1_t[:, tile_slice(i)] = nn(wup[1], g[...]).astype(BF16)

            extra = (square_part(AU1, column(u1_t, i)), [], [], [up])[r]
            return (symmetric_part(AD1, h, r) + rectangle_part(DD1, turned(grad, i), h, r)
                    + rectangle_part(DU1, column(u1_t, i), g, r) + extra)

        row_pass(first, second, PLAN_2A, store=True)

    def pass_2b():
        square_pass(SU1, PLAN_2B)

    def pass_3a():
        def first(i, r, h, g):
            return activation_part(0, r, turned(tok, i), column(e1_t, i), h, g)

        def second(i, r, h, g):
            extra = square_part(SD0, column(e1_t, i)) if r == 0 else []
            return extra + rectangle_part(DD0, column(e1_t, i), h, r) + rectangle_part(DU0, turned(tok, i), g, r)

        row_pass(first, second, PLAN_3A, store=True)

    def pass_3b():
        square_pass(SU0, PLAN_3B)

    def square_pass(base, plan):
        last = tiles // 2 - 1

        def g_in(m, k):
            slot = 2 * lax.rem(m, 2) + k
            return pltpu.make_async_copy(g_hbm.at[2 * m + k], hg.at[slot], g_sem.at[slot])

        def body(m, carry):
            @pl.when(m >= 1)
            def _():
                for k in range(2):
                    g_in(m - 1, k).wait()

            @pl.when(m < last)
            def _():
                for k in range(2):
                    g_in(m, k).start()

            slot = 2 * lax.rem(m + 1, 2)
            both = [hg.at[slot], hg.at[slot + 1]]
            for r in range(4):
                for j in COLUMNS[r]:
                    add_column(base, both, j)
            ticks(m, plan)
            return carry

        lax.fori_loop(0, last + 1, body, 0)

    def steps(plan):
        for u, step in plan:
            advance(u, step)

    pass_1()
    pl.semaphore_wait(barrier, 3)
    pltpu.make_async_copy(big_old, big_old, old_sem.at[0]).wait()
    pltpu.make_async_copy(small_old, small_old, old_sem.at[1]).wait()
    pltpu.make_async_copy(corner_old, corner_old, old_sem.at[2]).wait()
    steps(AFTER_1)
    pass_2a()
    steps(AFTER_2A)
    pass_2b()
    steps(AFTER_2B)
    pass_3a()
    steps(AFTER_3A)
    pass_3b()
    steps(AFTER_3B)
    steps(TAIL)


def symmetric_block(g, base, row, col):
    if row < col:
        return g[base + ABOVE.index((row, col))]
    if row > col:
        return g[base + ABOVE.index((col, row))].T
    if row < 3:
        top = g[base + 6 + row, 0:128, :]
        right = g[base + 6 + row, 128:256, 128:256]
    else:
        top = jnp.concatenate([g[base + 6, 128:256, 0:128], g[base + 7, 128:256, 0:128]], axis=1)
        right = g[base + 8, 128:256, 0:128]
    return jnp.concatenate([top, jnp.concatenate([top[:, 128:256].T, right], axis=1)], axis=0)


def assemble_kernel(g, a_inv_hbm, s_inv_hbm, p_up, p_down, a_up, s_up, a_down, s_down, a_inv, s_inv, sem):
    b = pl.program_id(0)
    i = pl.program_id(1)
    copies = (pltpu.make_async_copy(a_inv_hbm, a_inv, sem.at[0]), pltpu.make_async_copy(s_inv_hbm, s_inv, sem.at[1]))

    @pl.when(jnp.logical_and(b == 0, i == 0))
    def _():
        for copy in copies:
            copy.start()

    @pl.when(jnp.logical_and(b == 0, i == 1))
    def _():
        for copy in copies:
            copy.wait()

    au, sd, ad, su, du, dd = (pair[0] + b * (pair[1] - pair[0]) for pair in (AU, SD, AD, SU, DU, DD))
    for row in range(4):
        @pl.when(i == row)
        def _():
            for j in range(4):
                cols = slice(j * 256, j * 256 + 256)
                a_down[0, :, cols] = symmetric_block(g, ad, row, j)
                s_up[0, :, cols] = symmetric_block(g, su, row, j)
            if row == 0:
                a_up[0] = g[au]
                s_down[0] = g[sd]
            if row == 1:
                for j in range(4):
                    p_up[0, :, j * 256:j * 256 + 256] = nn(a_inv[b], g[du + j], HIGHEST)
            if row == 2:
                for j in range(4):
                    p_down[0, j * 256:j * 256 + 256, :] = nn(g[dd + j].T, s_inv[b], HIGHEST)


def solution(mesh):
    shards = mesh.shape["data"]
    vmem = pltpu.VMEM
    whole = pl.BlockSpec(memory_space=vmem)
    anywhere = pl.BlockSpec(memory_space=pl.ANY)
    hbm = pl.BlockSpec(memory_space=pltpu.HBM)

    def local_step(tokens, out_grad, w_up, w_down, a_up_old, s_up_old, a_down_old, s_down_old,
                   a_up_inv, s_up_inv, a_down_inv, s_down_inv, factor_decay):
        rows = tokens.shape[0]
        tiles = rows // TILE
        dma = pltpu.SemaphoreType.DMA
        sums, _ = pl.pallas_call(
            functools.partial(main_kernel, rows, rows * shards),
            out_shape=(vmem((BLOCKS, 256, 256), F32), jax.ShapeDtypeStruct((tiles, FF, TILE), BF16)),
            in_specs=[anywhere, anywhere, whole, whole, pl.BlockSpec(memory_space=pltpu.SMEM)] + [anywhere] * 6,
            out_specs=(whole, anywhere),
            scratch_shapes=[
                vmem((rows, D), BF16), vmem((rows, D), BF16),
                vmem((2, FF, D), BF16), vmem((D, FF), BF16),
                vmem((D, rows), BF16), vmem((D, rows), BF16), vmem((4, FF, TILE), BF16),
                vmem((2, 256, TILE), BF16), vmem((2, 256, TILE), BF16), vmem((32, FF), F32),
                vmem((2, 2, 3, 32, FF), F32), vmem((2, 2, 3, 32, 128), F32), vmem((2, 2, 32, D), F32), vmem((2, FF, FF), F32),
                vmem((POOL, 128, 256), F32), vmem((2, POOL, 32, 256), F32), vmem((2, POOL, 16, 256), F32),
                dma((tiles,)), dma((tiles,)), dma((3,)), dma((2,)), dma((4,)),
                dma((len(UNITS), 10)), dma((len(UNITS), 10)),
                pltpu.SemaphoreType.REGULAR((len(UNITS), 5)),
            ],
            compiler_params=pltpu.CompilerParams(collective_id=0, has_side_effects=True,
                                                 vmem_limit_bytes=195 * 2 ** 18),
            name="passes_and_sums",
        )(tokens, out_grad, w_up, w_down, factor_decay.reshape(1, 1), a_up_old, s_up_old, a_down_old, s_down_old,
          s_up_inv, a_down_inv)

        def layer_rows(r, c):
            return pl.BlockSpec((1, r, c), lambda b, i: (b, i, 0))

        def layer_whole(r, c):
            return pl.BlockSpec((1, r, c), lambda b, i: (b, 0, 0))

        shape = jax.ShapeDtypeStruct
        return tuple(pl.pallas_call(
            assemble_kernel,
            grid=(2, 4),
            out_shape=(shape((2, D, FF), F32), shape((2, FF, D), F32), shape((2, D, D), F32),
                       shape((2, FF, FF), F32), shape((2, FF, FF), F32), shape((2, D, D), F32)),
            in_specs=[whole, hbm, hbm],
            out_specs=(layer_whole(D, FF), layer_whole(FF, D), layer_whole(D, D), layer_rows(256, FF),
                       layer_rows(256, FF), layer_whole(D, D)),
            scratch_shapes=[vmem((2, D, D), F32), vmem((2, D, D), F32), dma((2,))],
            compiler_params=pltpu.CompilerParams(vmem_limit_bytes=24 * 2 ** 20),
            name="write_outputs",
        )(sums, a_up_inv, s_down_inv))

    batch_spec = P("data", None)
    replicated = P()
    return jax.shard_map(local_step, mesh=mesh, in_specs=(batch_spec, batch_spec) + (replicated,) * 11,
                         out_specs=(replicated,) * 6, check_vma=False)
```

profile of v0, /device:TPU:0, one launch (start us, length us, event | category | flops | bytes accessed | tf_op | source)
XLA Modules:
  0.0 199.2 jit_solution(7103587312607289942)
XLA Ops:
  1.3 0.0 copy-start
  1.3 0.0 copy-start.1
  1.3 186.7 %passes_and_sums.1 = (f32[56,256,256]{2,1,0:T(8,128)S(1)}, bf16[16,1024,512]{2,1,0:T(8,128)(2,1)}) custom-call(bf16[8192,256]{1,0:T(8,128)(2,1)} %tok_hbm.1, bf16[8192,256]{1,0:T(8,128)(2,1)} %grad_hbm.1, bf16[2,256,1024]{2,1,0:T(8,128)(2,1)} %wup.1, bf16[2,1024,256]{2,1,0:T(8,128)(2,1)} %wdn.1, f32[1,1]{1,0:T(1,128)} %bitcast.1.rho_ref, ...), custom_call_target="tpu_custom_call" | custom-call | tf_op jit(solution)/shard_map/passes_and_sums/pallas_call | solution.py:529
  188.0 0.0 copy-done
  188.0 0.0 copy-done.1
  188.0 11.0 %write_outputs.1 = (f32[2,256,1024]{2,1,0:T(8,128)}, f32[2,1024,256]{2,1,0:T(8,128)}, f32[2,256,256]{2,1,0:T(8,128)}, f32[2,1024,1024]{2,1,0:T(8,128)}, f32[2,10...) custom-call(f32[56,256,256]{2,1,0:T(8,128)S(1)} %get-tuple-element.7.g, f32[2,256,256]{2,1,0:T(8,128)S(1)} %copy-done, ...), custom_call_target="tpu_custom_call" | custom-call | tf_op jit(solution)/shard_map/write_outputs/pallas_call | solution.py:558
Async XLA Ops:
  1.3 186.7 %copy-start = (f32[2,256,256]{2,1,0:T(8,128)S(1)}, f32[2,256,256]{2,1,0:T(8,128)}, u32[]{:S(2)}) copy-start(f32[2,256,256]{2,1,0:T(8,128)} %a_inv_hbm.1) | copy-start | bytes 1572868
  1.3 186.7 %copy-start.1 = (f32[2,256,256]{2,1,0:T(8,128)S(1)}, f32[2,256,256]{2,1,0:T(8,128)}, u32[]{:S(2)}) copy-start(f32[2,256,256]{2,1,0:T(8,128)} %s_inv_hbm.1) | copy-start | bytes 1572868
where the time goes:
time: 199 us
  Pallas kernels  198 us (99%)
    pallas_call x1, Pallas kernels, local_step(): pl.pallas_call(functools.partial(main_kernel, rows, rows * shards), out_s...  187 us
    pallas_call x1, Pallas kernels, local_step(): pl.pallas_call(assemble_kernel, grid=(2, 4), out_shape=(shape((2, D, FF),...  11 us

commit v1 on v0

v1 whole, which is shorter than its diff:
```python
import functools

import jax
import jax.numpy as jnp
from jax import lax
from jax.experimental import pallas as pl
from jax.experimental.pallas import tpu as pltpu
from jax.sharding import PartitionSpec as P

F32 = jnp.float32
BF16 = jnp.bfloat16
MESH = pl.DeviceIdType.MESH
HIGHEST = lax.Precision.HIGHEST
PIECE = 16
SHARE = 0.0

D = 256
HALF = 128
QUAD = 64
PAIR = 32
OWN = 16
FF = 1024
TILE = 512
C0 = 0.7978845608028654
C1 = C0 * 0.044715

AU0, SD1, AD0, AU1, AD1, DD1, DU1, SU1, SD0, DU0, DD0, SU0 = 0, 1, 2, 11, 12, 21, 25, 29, 38, 39, 43, 47
BLOCKS = 56
AU = (AU0, AU1)
SD = (SD0, SD1)
AD = (AD0, AD1)
SU = (SU0, SU1)
DU = (DU0, DU1)
DD = (DD0, DD1)
ABOVE = ((0, 1), (0, 2), (1, 2), (0, 3), (1, 3), (2, 3))
LAST = ((0, 0), (0, 1), (1, 1))
COLUMNS = ((0, 1), (2,), (3,), ())

UNITS = ((0, 11, 0), (11, 10, 11), (21, 4, 21), (25, 4, 25), (29, 9, 0), (38, 5, 11), (43, 4, 16), (47, 3, 21), (50, 3, 24), (53, 3, 27))
POOL = 30

AFTER_1 = (0,)
PLAN_2A = (300, 700, 1000, 1400)
AFTER_2A = (1, 3, 2)
PLAN_2B = (201, 400, 402, 503, 700)
AFTER_2B = (4,)
PLAN_3A = (1, 104, 102, 401, 503, 602, 704, 801, 803, 1004, 1102, 1201, 1203, 1401, 1404)
AFTER_3A = (6, 5)
PLAN_3B = (106, 205, 302, 503, 606, 602)
AFTER_3B = (7,)
TAIL = (3, 8, 9, 5, 7, 8, 5, 9, 7, 4, 6, 8, 9, 6, 8, 7, 5, 9, 4, 6, 7, 8, 9, 5, 5, 7, 8, 7, 6, 8, 9, 9)


def next_steps():
    taken = [0] * len(UNITS)
    found = []
    for plan in (AFTER_1, PLAN_2A, AFTER_2A, PLAN_2B, AFTER_2B, PLAN_3A, AFTER_3A, PLAN_3B, AFTER_3B, TAIL):
        steps = []
        for code in plan:
            unit = code % 100
            steps.append((code // 100, unit, taken[unit]))
            taken[unit] += 1
        found.append(steps)
    return found


STEPS = next_steps()


def block_kinds():
    kinds = {}
    for b in range(2):
        for m, base in enumerate((AD[b], SU[b])):
            for k, (i, j) in enumerate(ABOVE):
                kinds[base + k] = ("above", m, b, i, j)
            for k in range(3):
                kinds[base + 6 + k] = ("diagonal", m, b, k, k)
        kinds[AU[b]] = ("small", 0, b, 0, 0)
        kinds[SD[b]] = ("small", 1, b, 0, 0)
    return kinds


KINDS = block_kinds()


def nn(a, b, precision=None):
    return lax.dot_general(a, b, (((1,), (0,)), ((), ())), preferred_element_type=F32, precision=precision)


def nt(a, b):
    return lax.dot_general(a, b, (((1,), (1,)), ((), ())), preferred_element_type=F32)


def thirds(x):
    high = x.astype(BF16)
    rest = x - high.astype(F32)
    mid = rest.astype(BF16)
    return high, mid, (rest - mid.astype(F32)).astype(BF16)


def half_gelu(z):
    sq = z * z
    return sq, jnp.tanh(z * (C1 * sq + C0)) * 0.5 + 0.5


def main_kernel(rows, batch_total,
                tok_hbm, grad_hbm, wup, wdn, rho_ref, a_up_old, s_up_old, a_down_old, s_down_old, s_up_inv, a_down_inv,
                acc, g_hbm, tok, grad, wup_t, wdn_t, u1_t, e1_t, hg, z_part, dh_part, left, big_old, corner_old, small_old, inv,
                r0, r1, r2, tok_sem, grad_sem, old_sem, inv_sem, g_sem, send_sem, recv_sem, sent_sem):
    tiles = rows // TILE
    me = lax.axis_index("data")
    core = lax.rem(me, 2)
    xpos = lax.rem(me // 2, 2)
    ypos = me // 4
    core_peer = me + 1 - 2 * core
    x_peer = me + 2 - 4 * xpos
    y_peer = me + 4 - 8 * ypos

    barrier = pltpu.get_barrier_semaphore()
    for peer in (core_peer, x_peer, y_peer):
        pl.semaphore_signal(barrier, inc=1, device_id=(peer,), device_id_type=MESH)

    def tok_copy(i):
        ds = pl.ds(i * TILE, TILE)
        return pltpu.make_async_copy(tok_hbm.at[ds, :], tok.at[ds, :], tok_sem.at[i])

    def grad_copy(i):
        ds = pl.ds(i * TILE, TILE)
        return pltpu.make_async_copy(grad_hbm.at[ds, :], grad.at[ds, :], grad_sem.at[i])

    for i in range(tiles):
        tok_copy(i).start()
        grad_copy(i).start()

    half = core * HALF
    a_half = half + xpos * PAIR
    b_half = half + QUAD + ypos * PAIR
    own_a = a_half + ypos * OWN
    own_b = b_half + xpos * OWN
    own = (own_a, own_b)

    for m, old in enumerate((a_down_old, s_up_old)):
        for b in range(2):
            for i in range(3):
                for p in range(2):
                    dst = pl.ds(p * OWN, OWN)
                    pltpu.make_async_copy(old.at[b, pl.ds(i * D + own[p], OWN), :],
                                          big_old.at[m, b, i, dst, :], old_sem.at[0]).start()
                    row = i * D + own[p] + core * (768 + HALF * LAST[i][0] - HALF - i * D)
                    col = i * D + core * (768 + HALF * LAST[i][1] - i * D)
                    pltpu.make_async_copy(old.at[b, pl.ds(pl.multiple_of(row, OWN), OWN), pl.ds(pl.multiple_of(col, HALF), HALF)],
                                          corner_old.at[m, b, i, dst, :], old_sem.at[2]).start()
    for m, old in enumerate((a_up_old, s_down_old)):
        for b in range(2):
            for p in range(2):
                pltpu.make_async_copy(old.at[b, pl.ds(own[p], OWN), :],
                                      small_old.at[m, b, pl.ds(p * OWN, OWN), :], old_sem.at[1]).start()

    def inv_copy(slot, b):
        return pltpu.make_async_copy((s_up_inv, a_down_inv)[slot].at[b], inv.at[slot], inv_sem.at[slot])

    for slot in range(2):
        inv_copy(slot, 1).start()

    acc[...] = jnp.zeros_like(acc)
    for b in range(2):
        wup_t[b] = wup[b].T
    wdn_t[...] = wdn[0].T

    def remote(u, slot, src, dst, peer):
        return pltpu.make_async_remote_copy(src_ref=src, dst_ref=dst, send_sem=send_sem.at[u, slot],
                                            recv_sem=recv_sem.at[u, slot], device_id=(peer,), device_id_type=MESH)

    def exchange(u, stage):
        b0, n, p0 = UNITS[u]
        blk = pl.ds(b0, n)
        pool = pl.ds(p0, n)

        def at(row, count):
            return acc.at[blk, pl.ds(pl.multiple_of(row, OWN), count), :]

        if stage == 0:
            return [remote(u, 0, at((1 - core) * HALF, HALF), r0.at[pool], core_peer)]
        if stage == 1:
            return [remote(u, 1, at(half + (1 - xpos) * PAIR, PAIR), r1.at[0, pool], x_peer),
                    remote(u, 2, at(half + QUAD + (1 - ypos) * PAIR, PAIR), r1.at[1, pool], y_peer)]
        if stage == 2:
            return [remote(u, 3, at(a_half + (1 - ypos) * OWN, OWN), r2.at[0, pool], y_peer),
                    remote(u, 4, at(b_half + (1 - xpos) * OWN, OWN), r2.at[1, pool], x_peer)]
        if stage == 3:
            return [remote(u, 5, at(own_a, OWN), at(own_a, OWN), y_peer),
                    remote(u, 6, at(own_b, OWN), at(own_b, OWN), x_peer)]
        if stage == 4:
            return [remote(u, 7, at(a_half, PAIR), at(a_half, PAIR), x_peer),
                    remote(u, 8, at(b_half, PAIR), at(b_half, PAIR), y_peer)]
        return [remote(u, 9, at(half, HALF), at(half, HALF), core_peer)]

    slots = {0: [(0, core_peer)], 1: [(1, x_peer), (2, y_peer)], 2: [(3, y_peer), (4, x_peer)]}

    def start(u, stage):
        if stage >= 3:
            for slot, _ in slots[5 - stage]:
                pl.semaphore_wait(sent_sem.at[u, slot], 1)
        for copy in exchange(u, stage):
            copy.start()

    def finish(u, stage):
        for copy in exchange(u, stage):
            copy.wait()
        if stage < 3:
            for slot, peer in slots[stage]:
                pl.semaphore_signal(sent_sem.at[u, slot], inc=1, device_id=(peer,), device_id_type=MESH)

    def add_rows(u, row, count, buf, lead):
        b0, n, p0 = UNITS[u]
        ds = pl.ds(pl.multiple_of(row, OWN), count)

        def body(k, carry):
            acc[b0 + k, ds, :] += buf[lead + (p0 + k,)]
            return carry

        lax.fori_loop(0, n, body, 0)

    def factor_update(u):
        b0, n, _ = UNITS[u]
        rho = rho_ref[0, 0]
        fresh = (1.0 - rho) * (1.0 / batch_total)
        for k in range(b0, b0 + n):
            if k not in KINDS:
                continue
            kind, m, b, i, j = KINDS[k]
            for p in range(2):
                ds = pl.ds(pl.multiple_of(own[p], OWN), OWN)
                if kind == "small":
                    parts = [(slice(0, D), small_old[m, b, p * OWN:p * OWN + OWN, :])]
                elif kind == "above":
                    parts = [(slice(0, D), big_old[m, b, i, p * OWN:p * OWN + OWN, j * D:j * D + D])]
                else:
                    parts = [(slice(0, HALF), corner_old[m, b, i, p * OWN:p * OWN + OWN, :]),
                             (slice(HALF, D), big_old[m, b, i, p * OWN:p * OWN + OWN, i * D + HALF:i * D + D])]
                for cols, old in parts:
                    acc[k, ds, cols] = rho * old + fresh * acc[k, ds, cols]

    def wide_product(first, slot):
        ds = [pl.ds(pl.multiple_of(own[p], OWN), OWN) for p in range(2)]
        for j in range(4):
            for p in range(2):
                parts = thirds(acc[first + j, ds[p], :] * (1.0 / batch_total))
                for n, part in enumerate(parts):
                    left[n * PAIR + p * OWN:n * PAIR + p * OWN + OWN, j * D:j * D + D] = part

        def body(j, carry):
            high, mid, low = thirds(inv[slot, :, pl.ds(pl.multiple_of(j * D, D), D)])
            by_high = nn(left[...], high)
            by_mid = nn(left[0:QUAD, :], mid)
            prod = ((by_high[QUAD:96, :] + nn(left[0:PAIR, :], low) + by_mid[PAIR:QUAD, :])
                    + (by_high[PAIR:QUAD, :] + by_mid[0:PAIR, :])) + by_high[0:PAIR, :]
            for p in range(2):
                acc[first + j, ds[p], :] = prod[p * OWN:p * OWN + OWN, :]
            return carry

        lax.fori_loop(0, 4, body, 0)

    def post(u):
        b0, n, _ = UNITS[u]
        factor_update(u)
        for b in (1, 0):
            for slot, first in enumerate((DU[b], DD[b])):
                if b0 <= first < b0 + n:
                    inv_copy(slot, b).wait()
                    wide_product(first, slot)
                    if b == 1:
                        inv_copy(slot, 0).start()

    def advance(u, step):
        if step == 0:
            start(u, 0)
            return
        finish(u, step - 1)
        if step == 1:
            add_rows(u, half, HALF, r0, ())
        elif step == 2:
            add_rows(u, a_half, PAIR, r1, (0,))
            add_rows(u, b_half, PAIR, r1, (1,))
        elif step == 3:
            add_rows(u, own_a, OWN, r2, (0,))
            add_rows(u, own_b, OWN, r2, (1,))
            post(u)
        if step < 6:
            start(u, step)

    def ticks(m, plan, per_step=1, k=0):
        for t in sorted(set(t for t, _, _ in plan)):
            if t % per_step != k:
                continue

            @pl.when(m == t // per_step)
            def _():
                for when, u, step in plan:
                    if when == t:
                        advance(u, step)

    def add_column(base, refs, j, lo=0):
        prod = sum(nt(ref[lo * D:j * D + D, :], ref[j * D:j * D + D, :]) for ref in refs)
        for i in range(lo, j):
            acc[base + ABOVE.index((i, j))] += prod[(i - lo) * D:(i - lo) * D + D, :]
        prod = prod[(j - lo) * D:(j - lo) * D + D, :]
        if j < 3:
            acc[base + 6 + j, 0:HALF, :] += prod[0:HALF, :]
            acc[base + 6 + j, HALF:D, HALF:D] += prod[HALF:D, HALF:D]
        else:
            for k, (m, n) in enumerate(LAST):
                acc[base + 6 + k, HALF:D, 0:HALF] += prod[m * HALF:m * HALF + HALF, n * HALF:n * HALF + HALF]

    def symmetric_part(base, ref, r):
        return [(j + 1, functools.partial(add_column, base, [ref], j)) for j in COLUMNS[r]]

    def rectangle_part(base, left, ref, r):
        def add():
            acc[base + r] += nt(left(), ref[r * D:r * D + D, :])

        return [(1, add)]

    def square_part(base, x):
        def add():
            acc[base] += nt(x(), x())

        return [(1, add)]

    def activation_part(b, r, u_t, q_t, h, g):
        z_ref, dh_ref = z_part.at[r % 2], dh_part.at[r % 2]

        def products():
            z_ref[...] = nn(wup_t[b, r * D:r * D + D, :], u_t()).astype(BF16)
            if g is not None:
                dh_ref[...] = nn(wdn[b, r * D:r * D + D, :], q_t()).astype(BF16)

        def piece(k):
            rows_in = slice(k * PIECE, k * PIECE + PIECE)
            rows_out = slice(r * D + k * PIECE, r * D + k * PIECE + PIECE)
            z = z_ref[rows_in, :].astype(F32)
            sq, s = half_gelu(z)
            if h is not None:
                h[rows_out, :] = (z * s).astype(BF16)
            if g is not None:
                slope = s + (z * (s - s * s)) * (6 * C1 * sq + 2 * C0)
                g[rows_out, :] = (dh_ref[rows_in, :].astype(F32) * slope).astype(BF16)

        return [(0, products)] + [(1, functools.partial(piece, k)) for k in range(D // PIECE)]

    def ahead(quarters):
        order = [quarters[0][0]]
        for r in range(4):
            if r < 3:
                order.append(quarters[r + 1][0])
            order += quarters[r][1:]
        return order

    def interleave(one, two):
        order = []
        for n, parts in enumerate((one, two)):
            total, before = sum(cost for cost, _ in parts), 0
            for cost, part in parts:
                order.append(((before + SHARE * cost) / total, n, len(order), part))
                before += cost
        for _, _, _, part in sorted(order, key=lambda entry: entry[:3]):
            part()

    def tile_slice(i):
        return pl.ds(pl.multiple_of(i * TILE, TILE), TILE)

    def row_pass(first, second, plan, begin=None, store=False):
        pairs = ((hg.at[0], hg.at[2]), (hg.at[1], hg.at[3]))

        def out(i, k):
            return pltpu.make_async_copy(pairs[k][1], g_hbm.at[i], g_sem.at[k])

        if begin is not None:
            begin(0)
        for r in range(4):
            for _, part in first(0, r, *pairs[0]):
                part()

        def body(m, carry):
            for k in range(2):
                i = 2 * m + k
                nxt = i + 1 if k == 0 else jnp.minimum(i + 1, tiles - 2)
                if store:
                    out(i, k).start()
                if begin is not None:
                    begin(i + 1)
                one = [first(nxt, r, *pairs[1 - k]) for r in range(4)]
                one = ahead(one)
                two = [part for r in range(4) for part in second(i, r, *pairs[k])]
                interleave(one, two)
                if store:
                    out(i, k).wait()
                ticks(m, plan, 2, k)
            return carry

        lax.fori_loop(0, tiles // 2, body, 0)

    def column(ref, i):
        return lambda: ref[:, tile_slice(i)]

    def turned(ref, i):
        return lambda: ref[tile_slice(i), :].T

    def pass_1():
        def begin(i):
            @pl.when(i < tiles)
            def _():
                tok_copy(i).wait()
                grad_copy(i).wait()

        def first(i, r, h, g):
            return activation_part(0, r, turned(tok, i), None, h, None)

        def second(i, r, h, g):
            def down():
                u1_t[:, tile_slice(i)] = nn(wdn_t[...], h[...]).astype(BF16)

            extra = ([(4, down)], square_part(AU0, turned(tok, i)), square_part(SD1, turned(grad, i)), [])[r]
            return extra + symmetric_part(AD0, h, r)

        row_pass(first, second, (), begin)

    def pass_2a():
        def first(i, r, h, g):
            return activation_part(1, r, column(u1_t, i), turned(grad, i), h, g)

        def second(i, r, h, g):
            def up():
                e1_t[:, tile_slice(i)] = nn(wup[1], g[...]).astype(BF16)

            extra = (square_part(AU1, column(u1_t, i)), [], [], [(4, up)])[r]
            return (symmetric_part(AD1, h, r) + rectangle_part(DD1, turned(grad, i), h, r)
                    + rectangle_part(DU1, column(u1_t, i), g, r) + extra)

        row_pass(first, second, STEPS[1], store=True)

    def pass_2b():
        square_pass(SU1, STEPS[3])

    def pass_3a():
        def first(i, r, h, g):
            return activation_part(0, r, turned(tok, i), column(e1_t, i), h, g)

        def second(i, r, h, g):
            extra = square_part(SD0, column(e1_t, i)) if r == 0 else []
            return extra + rectangle_part(DD0, column(e1_t, i), h, r) + rectangle_part(DU0, turned(tok, i), g, r)

        row_pass(first, second, STEPS[5], store=True)

    def pass_3b():
        square_pass(SU0, STEPS[7])

    def square_pass(base, plan):
        last = tiles // 2 - 1

        def g_in(m, k):
            slot = 2 * lax.rem(m, 2) + k
            return pltpu.make_async_copy(g_hbm.at[2 * m + k], hg.at[slot], g_sem.at[slot])

        def body(m, carry):
            @pl.when(m >= 1)
            def _():
                for k in range(2):
                    g_in(m - 1, k).wait()

            @pl.when(m < last)
            def _():
                for k in range(2):
                    g_in(m, k).start()

            slot = 2 * lax.rem(m + 1, 2)
            both = [hg.at[slot], hg.at[slot + 1]]
            for r in range(4):
                for j in COLUMNS[r]:
                    add_column(base, both, j)
            ticks(m, plan)
            return carry

        lax.fori_loop(0, last + 1, body, 0)

    def steps(plan):
        for _, u, step in plan:
            advance(u, step)

    pass_1()
    pl.semaphore_wait(barrier, 3)
    pltpu.make_async_copy(big_old, big_old, old_sem.at[0]).wait()
    pltpu.make_async_copy(small_old, small_old, old_sem.at[1]).wait()
    pltpu.make_async_copy(corner_old, corner_old, old_sem.at[2]).wait()
    steps(STEPS[0])
    pass_2a()
    steps(STEPS[2])
    pass_2b()
    steps(STEPS[4])
    pass_3a()
    steps(STEPS[6])
    pass_3b()
    steps(STEPS[8])
    steps(STEPS[9])


def assemble_kernel(g, a_inv, s_inv, p_up, p_down, a_up, s_up, a_down, s_down, turned, diagonal, up, down, sem):
    def starts(b):
        return [pair[0] + b * (pair[1] - pair[0]) for pair in (AU, SD, AD, SU, DU, DD)]

    def block(out, b, i, j):
        return out.at[b, pl.ds(i * D, D), pl.ds(j * D, D)]

    def copies(b):
        au, sd, ad, su, _, _ = starts(b)
        groups = [[(g.at[au], a_up.at[b]), (g.at[sd], s_down.at[b])], [], [], [(up.at[b], p_up.at[b]), (down.at[b], p_down.at[b])]]
        for m, (out, base) in enumerate(((a_down, ad), (s_up, su))):
            for k, (i, j) in enumerate(ABOVE):
                groups[0].append((g.at[base + k], block(out, b, i, j)))
                groups[1].append((turned.at[b, m, k], block(out, b, j, i)))
            for i in range(4):
                groups[2].append((diagonal.at[b, m, i], block(out, b, i, i)))
        slot = iter(range(sum(map(len, groups))))
        return [[pltpu.make_async_copy(src, dst, sem.at[b, next(slot)]) for src, dst in group] for group in groups]

    def start(b, group):
        for copy in copies(b)[group]:
            copy.start()

    def plain(b, carry):
        start(b, 0)
        return carry

    def mirror(b, carry):
        _, _, ad, su, _, _ = starts(b)
        for m, base in enumerate((ad, su)):
            for k in range(len(ABOVE)):
                turned[b, m, k] = g[base + k].T
        start(b, 1)
        for m, base in enumerate((ad, su)):
            for i in range(4):
                if i < 3:
                    top = g[base + 6 + i, 0:HALF, :]
                    right = g[base + 6 + i, HALF:D, HALF:D]
                else:
                    top = jnp.concatenate([g[base + 6, HALF:D, 0:HALF], g[base + 7, HALF:D, 0:HALF]], axis=1)
                    right = g[base + 8, HALF:D, 0:HALF]
                diagonal[b, m, i, 0:HALF, :] = top
                diagonal[b, m, i, HALF:D, 0:HALF] = top[:, HALF:D].T
                diagonal[b, m, i, HALF:D, HALF:D] = right
        start(b, 2)
        return carry

    def products(b, carry):
        _, _, _, _, du, dd = starts(b)
        for j in range(4):
            cols = slice(j * D, j * D + D)
            up[b, :, cols] = nn(a_inv[b], g[du + j], HIGHEST)
            down[b, cols, :] = nn(g[dd + j].T, s_inv[b], HIGHEST)
        start(b, 3)
        return carry

    def finish(b, carry):
        for group in copies(b):
            for copy in group:
                copy.wait()
        return carry

    for stage in (plain, mirror, products, finish):
        lax.fori_loop(0, 2, stage, 0)


def solution(mesh):
    shards = mesh.shape["data"]
    vmem = pltpu.VMEM
    whole = pl.BlockSpec(memory_space=vmem)
    anywhere = pl.BlockSpec(memory_space=pl.ANY)

    def local_step(tokens, out_grad, w_up, w_down, a_up_old, s_up_old, a_down_old, s_down_old,
                   a_up_inv, s_up_inv, a_down_inv, s_down_inv, factor_decay):
        rows = tokens.shape[0]
        tiles = rows // TILE
        dma = pltpu.SemaphoreType.DMA
        sums, _ = pl.pallas_call(
            functools.partial(main_kernel, rows, rows * shards),
            out_shape=(vmem((BLOCKS, D, D), F32), jax.ShapeDtypeStruct((tiles, FF, TILE), BF16)),
            in_specs=[anywhere, anywhere, whole, whole, pl.BlockSpec(memory_space=pltpu.SMEM)] + [anywhere] * 6,
            out_specs=(whole, anywhere),
            scratch_shapes=[
                vmem((rows, D), BF16), vmem((rows, D), BF16),
                vmem((2, FF, D), BF16), vmem((D, FF), BF16),
                vmem((D, rows), BF16), vmem((D, rows), BF16), vmem((4, FF, TILE), BF16),
                vmem((2, D, TILE), BF16), vmem((2, D, TILE), BF16), vmem((96, FF), BF16),
                vmem((2, 2, 3, PAIR, FF), F32), vmem((2, 2, 3, PAIR, HALF), F32), vmem((2, 2, PAIR, D), F32), vmem((2, FF, FF), F32),
                vmem((POOL, HALF, D), F32), vmem((2, POOL, PAIR, D), F32), vmem((2, POOL, OWN, D), F32),
                dma((tiles,)), dma((tiles,)), dma((3,)), dma((2,)), dma((4,)),
                dma((len(UNITS), 10)), dma((len(UNITS), 10)),
                pltpu.SemaphoreType.REGULAR((len(UNITS), 5)),
            ],
            compiler_params=pltpu.CompilerParams(collective_id=0, has_side_effects=True,
                                                 vmem_limit_bytes=195 * 2 ** 18),
            name="passes_and_sums",
        )(tokens, out_grad, w_up, w_down, factor_decay.reshape(1, 1), a_up_old, s_up_old, a_down_old, s_down_old,
          s_up_inv, a_down_inv)

        shape = jax.ShapeDtypeStruct
        return tuple(pl.pallas_call(
            assemble_kernel,
            out_shape=(shape((2, D, FF), F32), shape((2, FF, D), F32), shape((2, D, D), F32),
                       shape((2, FF, FF), F32), shape((2, FF, FF), F32), shape((2, D, D), F32)),
            in_specs=[whole] * 3,
            out_specs=(anywhere,) * 6,
            scratch_shapes=[vmem((2, 2, 6, D, D), F32), vmem((2, 2, 4, D, D), F32), vmem((2, D, FF), F32),
                            vmem((2, FF, D), F32), dma((2, 36))],
            compiler_params=pltpu.CompilerParams(vmem_limit_bytes=24 * 2 ** 20),
            name="write_outputs",
        )(sums, a_up_inv, s_down_inv))

    batch_spec = P("data", None)
    replicated = P()
    return jax.shard_map(local_step, mesh=mesh, in_specs=(batch_spec, batch_spec) + (replicated,) * 11,
                         out_specs=(replicated,) * 6, check_vma=False)
```

time: 199 us -> 193 us (0.970)
  Pallas kernels: 198 us -> 192 us
    pallas_call x1, Pallas kernels: 11 us -> 8.08 us  [local_step(): pl.pallas_call(assemble_kernel, out_shape=(shape((2, D, FF), F32), shape(...]
    pallas_call x1, Pallas kernels: 187 us -> 184 us  [local_step(): pl.pallas_call(functools.partial(main_kernel, rows, rows * shards), out_s...]
where the time goes in v1:
time: 193 us
  Pallas kernels  192 us (99%)
    pallas_call x1, Pallas kernels, local_step(): pl.pallas_call(functools.partial(main_kernel, rows, rows * shards), out_s...  184 us
    pallas_call x1, Pallas kernels, local_step(): pl.pallas_call(assemble_kernel, out_shape=(shape((2, D, FF), F32), shape(...  8.08 us

profile of v1, /device:TPU:0, one launch (start us, length us, event | category | flops | bytes accessed | tf_op | source)
XLA Modules:
  0.0 193.4 jit_solution(4393779492360071941)
XLA Ops:
  1.3 0.0 copy-start
  1.3 0.0 copy-start.1
  1.3 183.8 %passes_and_sums.1 = (f32[56,256,256]{2,1,0:T(8,128)S(1)}, bf16[16,1024,512]{2,1,0:T(8,128)(2,1)}) custom-call(bf16[8192,256]{1,0:T(8,128)(2,1)} %tok_hbm.1, bf16[8192,256]{1,0:T(8,128)(2,1)} %grad_hbm.1, bf16[2,256,1024]{2,1,0:T(8,128)(2,1)} %wup.1, bf16[2,1024,256]{2,1,0:T(8,128)(2,1)} %wdn.1, f32[1,1]{1,0:T(1,128)} %bitcast.1.rho_ref, ...), custom_call_target="tpu_custom_call" | custom-call | tf_op jit(solution)/shard_map/passes_and_sums/pallas_call | solution.py:584
  185.1 0.0 copy-done
  185.1 0.0 copy-done.1
  185.1 8.1 %write_outputs.1 = (f32[2,256,1024]{2,1,0:T(8,128)}, f32[2,1024,256]{2,1,0:T(8,128)}, f32[2,256,256]{2,1,0:T(8,128)}, f32[2,1024,1024]{2,1,0:T(8,128)}, f32[2,10...) custom-call(f32[56,256,256]{2,1,0:T(8,128)S(1)} %get-tuple-element.7.g, f32[2,256,256]{2,1,0:T(8,128)S(1)} %copy-done, ...), custom_call_target="tpu_custom_call" | custom-call | tf_op jit(solution)/shard_map/write_outputs/pallas_call | solution.py:607
Async XLA Ops:
  1.3 183.8 %copy-start = (f32[2,256,256]{2,1,0:T(8,128)S(1)}, f32[2,256,256]{2,1,0:T(8,128)}, u32[]{:S(2)}) copy-start(f32[2,256,256]{2,1,0:T(8,128)} %a_inv.1) | copy-start | bytes 1572868
  1.3 183.8 %copy-start.1 = (f32[2,256,256]{2,1,0:T(8,128)S(1)}, f32[2,256,256]{2,1,0:T(8,128)}, u32[]{:S(2)}) copy-start(f32[2,256,256]{2,1,0:T(8,128)} %s_inv.1) | copy-start | bytes 1572868

commit v2 on v1

--- a/solution.py
+++ b/solution.py
@@ -40,15 +40,15 @@
 POOL = 30
 
 AFTER_1 = (0,)
-PLAN_2A = (300, 700, 1000, 1400)
-AFTER_2A = (1, 3, 2)
-PLAN_2B = (201, 400, 402, 503, 700)
+PLAN_2A = (200, 600, 900, 1300)
+AFTER_2A = (1, 2, 3)
+PLAN_2B = (201, 300, 303, 402, 600)
 AFTER_2B = (4,)
-PLAN_3A = (1, 104, 102, 401, 503, 602, 704, 801, 803, 1004, 1102, 1201, 1203, 1401, 1404)
+PLAN_3A = (1, 104, 202, 301, 303, 604, 801, 802, 904, 1003, 1101, 1202, 1301, 1303, 1404)
 AFTER_3A = (6, 5)
-PLAN_3B = (106, 205, 302, 503, 606, 602)
+PLAN_3B = (2, 202, 206, 205, 503, 606)
 AFTER_3B = (7,)
-TAIL = (3, 8, 9, 5, 7, 8, 5, 9, 7, 4, 6, 8, 9, 6, 8, 7, 5, 9, 4, 6, 7, 8, 9, 5, 5, 7, 8, 7, 6, 8, 9, 9)
+TAIL = (3, 8, 9, 5, 7, 8, 9, 6, 5, 7, 4, 8, 9, 6, 7, 8, 9, 5, 4, 6, 8, 9, 7, 5, 5, 8, 9, 9, 8, 6, 7, 7)
 
 
 def next_steps():
@@ -356,12 +356,15 @@
             order += quarters[r][1:]
         return order
 
-    def interleave(one, two):
+    def interleave(one, two, flat):
+        share = 0.5 if flat else SHARE
+        if flat:
+            one, two = ([(1, part) for _, part in parts] for parts in (one, two))
         order = []
         for n, parts in enumerate((one, two)):
             total, before = sum(cost for cost, _ in parts), 0
             for cost, part in parts:
-                order.append(((before + SHARE * cost) / total, n, len(order), part))
+                order.append(((before + share * cost) / total, n, len(order), part))
                 before += cost
         for _, _, _, part in sorted(order, key=lambda entry: entry[:3]):
             part()
@@ -369,7 +372,7 @@
     def tile_slice(i):
         return pl.ds(pl.multiple_of(i * TILE, TILE), TILE)
 
-    def row_pass(first, second, plan, begin=None, store=False):
+    def row_pass(first, second, plan, begin=None, store=False, flat=False):
         pairs = ((hg.at[0], hg.at[2]), (hg.at[1], hg.at[3]))
 
         def out(i, k):
@@ -392,7 +395,7 @@
                 one = [first(nxt, r, *pairs[1 - k]) for r in range(4)]
                 one = ahead(one)
                 two = [part for r in range(4) for part in second(i, r, *pairs[k])]
-                interleave(one, two)
+                interleave(one, two, flat)
                 if store:
                     out(i, k).wait()
                 ticks(m, plan, 2, k)
@@ -423,7 +426,7 @@
             extra = ([(4, down)], square_part(AU0, turned(tok, i)), square_part(SD1, turned(grad, i)), [])[r]
             return extra + symmetric_part(AD0, h, r)
 
-        row_pass(first, second, (), begin)
+        row_pass(first, second, (), begin, flat=True)
 
     def pass_2a():
         def first(i, r, h, g):

time: 193 us -> 192 us (level)
  no operation moved by 1% of the time
where the time goes in v2:
time: 192 us
  Pallas kernels  191 us (99%)
    pallas_call x1, Pallas kernels, local_step(): pl.pallas_call(functools.partial(main_kernel, rows, rows * shards), out_s...  182 us
    pallas_call x1, Pallas kernels, local_step(): pl.pallas_call(assemble_kernel, out_shape=(shape((2, D, FF), F32), shape(...  8.08 us

profile of v2, /device:TPU:0, one launch (start us, length us, event | category | flops | bytes accessed | tf_op | source)
XLA Modules:
  0.0 192.1 jit_solution(5322253837444407568)
XLA Ops:
  1.3 0.0 copy-start
  1.3 0.0 copy-start.1
  1.3 182.5 %passes_and_sums.1 = (f32[56,256,256]{2,1,0:T(8,128)S(1)}, bf16[16,1024,512]{2,1,0:T(8,128)(2,1)}) custom-call(bf16[8192,256]{1,0:T(8,128)(2,1)} %tok_hbm.1, bf16[8192,256]{1,0:T(8,128)(2,1)} %grad_hbm.1, bf16[2,256,1024]{2,1,0:T(8,128)(2,1)} %wup.1, bf16[2,1024,256]{2,1,0:T(8,128)(2,1)} %wdn.1, f32[1,1]{1,0:T(1,128)} %bitcast.1.rho_ref, ...), custom_call_target="tpu_custom_call" | custom-call | tf_op jit(solution)/shard_map/passes_and_sums/pallas_call | solution.py:587
  183.8 0.0 copy-done
  183.8 0.0 copy-done.1
  183.8 8.1 %write_outputs.1 = (f32[2,256,1024]{2,1,0:T(8,128)}, f32[2,1024,256]{2,1,0:T(8,128)}, f32[2,256,256]{2,1,0:T(8,128)}, f32[2,1024,1024]{2,1,0:T(8,128)}, f32[2,10...) custom-call(f32[56,256,256]{2,1,0:T(8,128)S(1)} %get-tuple-element.7.g, f32[2,256,256]{2,1,0:T(8,128)S(1)} %copy-done, ...), custom_call_target="tpu_custom_call" | custom-call | tf_op jit(solution)/shard_map/write_outputs/pallas_call | solution.py:610
Async XLA Ops:
  1.3 182.5 %copy-start = (f32[2,256,256]{2,1,0:T(8,128)S(1)}, f32[2,256,256]{2,1,0:T(8,128)}, u32[]{:S(2)}) copy-start(f32[2,256,256]{2,1,0:T(8,128)} %a_inv.1) | copy-start | bytes 1572868
  1.3 182.5 %copy-start.1 = (f32[2,256,256]{2,1,0:T(8,128)S(1)}, f32[2,256,256]{2,1,0:T(8,128)}, u32[]{:S(2)}) copy-start(f32[2,256,256]{2,1,0:T(8,128)} %s_inv.1) | copy-start | bytes 1572868

commit v3 on v2

--- a/solution.py
+++ b/solution.py
@@ -100,7 +100,8 @@
 
 def half_gelu(z):
     sq = z * z
-    return sq, jnp.tanh(z * (C1 * sq + C0)) * 0.5 + 0.5
+    t = jnp.tanh(z * (C1 * sq + C0))
+    return sq, t, t * 0.5 + 0.5
 
 
 def main_kernel(rows, batch_total,
@@ -339,11 +340,11 @@
             rows_in = slice(k * PIECE, k * PIECE + PIECE)
             rows_out = slice(r * D + k * PIECE, r * D + k * PIECE + PIECE)
             z = z_ref[rows_in, :].astype(F32)
-            sq, s = half_gelu(z)
+            sq, t, s = half_gelu(z)
             if h is not None:
                 h[rows_out, :] = (z * s).astype(BF16)
             if g is not None:
-                slope = s + (z * (s - s * s)) * (6 * C1 * sq + 2 * C0)
+                slope = s + (z * (1.0 - t * t)) * (1.5 * C1 * sq + 0.5 * C0)
                 g[rows_out, :] = (dh_ref[rows_in, :].astype(F32) * slope).astype(BF16)
 
         return [(0, products)] + [(1, functools.partial(piece, k)) for k in range(D // PIECE)]

time: 192 us -> 192 us (level)
  no operation moved by 1% of the time
where the time goes in v3:
time: 192 us
  Pallas kernels  191 us (99%)
    pallas_call x1, Pallas kernels, local_step(): pl.pallas_call(functools.partial(main_kernel, rows, rows * shards), out_s...  183 us
    pallas_call x1, Pallas kernels, local_step(): pl.pallas_call(assemble_kernel, out_shape=(shape((2, D, FF), F32), shape(...  8.08 us

profile of v3, /device:TPU:0, one launch (start us, length us, event | category | flops | bytes accessed | tf_op | source)
XLA Modules:
  0.0 192.2 jit_solution(14106653119750662856)
XLA Ops:
  1.3 0.0 copy-start
  1.3 0.0 copy-start.1
  1.3 182.6 %passes_and_sums.1 = (f32[56,256,256]{2,1,0:T(8,128)S(1)}, bf16[16,1024,512]{2,1,0:T(8,128)(2,1)}) custom-call(bf16[8192,256]{1,0:T(8,128)(2,1)} %tok_hbm.1, bf16[8192,256]{1,0:T(8,128)(2,1)} %grad_hbm.1, bf16[2,256,1024]{2,1,0:T(8,128)(2,1)} %wup.1, bf16[2,1024,256]{2,1,0:T(8,128)(2,1)} %wdn.1, f32[1,1]{1,0:T(1,128)} %bitcast.1.rho_ref, ...), custom_call_target="tpu_custom_call" | custom-call | tf_op jit(solution)/shard_map/passes_and_sums/pallas_call | solution.py:588
  183.9 0.0 copy-done
  183.9 0.0 copy-done.1
  183.9 8.1 %write_outputs.1 = (f32[2,256,1024]{2,1,0:T(8,128)}, f32[2,1024,256]{2,1,0:T(8,128)}, f32[2,256,256]{2,1,0:T(8,128)}, f32[2,1024,1024]{2,1,0:T(8,128)}, f32[2,10...) custom-call(f32[56,256,256]{2,1,0:T(8,128)S(1)} %get-tuple-element.7.g, f32[2,256,256]{2,1,0:T(8,128)S(1)} %copy-done, ...), custom_call_target="tpu_custom_call" | custom-call | tf_op jit(solution)/shard_map/write_outputs/pallas_call | solution.py:611
Async XLA Ops:
  1.3 182.6 %copy-start = (f32[2,256,256]{2,1,0:T(8,128)S(1)}, f32[2,256,256]{2,1,0:T(8,128)}, u32[]{:S(2)}) copy-start(f32[2,256,256]{2,1,0:T(8,128)} %a_inv.1) | copy-start | bytes 1572868
  1.3 182.6 %copy-start.1 = (f32[2,256,256]{2,1,0:T(8,128)S(1)}, f32[2,256,256]{2,1,0:T(8,128)}, u32[]{:S(2)}) copy-start(f32[2,256,256]{2,1,0:T(8,128)} %s_inv.1) | copy-start | bytes 1572868
